TPU v7x, 32 devices: a whole 2x2x4 slice. The times are simulated.
32 devices in a mesh: kt: 8 (over z, y), tile: 4 (over x, core).
Axes of the slice: x: 2, y: 2, z: 4, core: 2. Of those that a mesh axis runs over, the one named last changes fastest.
Arguments:
- green_particle: bfloat16 [2, 64, 1024, 1024], P(None, 'kt', 'tile'), may hold values from -6 to 6
- green_hole: bfloat16 [2, 64, 1024, 1024], P(None, 'kt', 'tile'), may hold values from -6 to 6
- coulomb: bfloat16 [2, 64, 1024, 1024], P(None, 'kt'), may hold values from -3 to 3
Outputs:
- screened: float32 [2, 64, 1024, 1024], P(None, 'kt', 'tile')
All inputs are finite; a program needn't handle non-finite values.
Results may differ from a plain program's by a relative error of at most 0.0039.
Values may be sent and summed in bfloat16 or wider, within the bound.
No kernel may reach another device: no remote copies, remote signals or barrier semaphores. Data moves between devices by JAX's collectives and lax.ppermute only.
A program may use at most 192 MiB of HBM per device.

v0:
```python
import math
import jax
import jax.numpy as jnp
from jax import lax
from jax.sharding import PartitionSpec as P

KSIDE = 4
K = 64
HIGHEST = lax.Precision.HIGHEST


def phase_tables(points, side_count):
    point_index = jnp.arange(points, dtype=jnp.int32)
    digit_high = point_index // (side_count * side_count)
    digit_mid = point_index // side_count % side_count
    digit_low = point_index % side_count
    phase_turns = (
        digit_high[:, None] * digit_high[None, :]
        + digit_mid[:, None] * digit_mid[None, :]
        + digit_low[:, None] * digit_low[None, :]
    ) % side_count
    angles = phase_turns.astype(jnp.float32) * (2.0 * math.pi / side_count)
    return (jnp.cos(angles) / points, jnp.sin(angles) / points)


def to_cells(real_part, imag_part, cosine_table, sine_table):
    return (
        jnp.dot(cosine_table, real_part, precision=HIGHEST)
        - jnp.dot(sine_table, imag_part, precision=HIGHEST),
        jnp.dot(sine_table, real_part, precision=HIGHEST)
        + jnp.dot(cosine_table, imag_part, precision=HIGHEST),
    )


def to_momenta(real_part, imag_part, cosine_table, sine_table):
    return (
        jnp.dot(cosine_table, real_part, precision=HIGHEST)
        + jnp.dot(sine_table, imag_part, precision=HIGHEST),
        jnp.dot(cosine_table, imag_part, precision=HIGHEST)
        - jnp.dot(sine_table, real_part, precision=HIGHEST),
    )


def polarize(particle, hole_part):
    cosine_table, sine_table = phase_tables(K, KSIDE)
    part_real, part_imag = to_cells(
        particle[0].astype(jnp.float32), particle[1].astype(jnp.float32), cosine_table, sine_table
    )
    hole_real, hole_imag = to_cells(
        hole_part[0].astype(jnp.float32), hole_part[1].astype(jnp.float32), cosine_table, sine_table
    )
    cell_real = part_real * hole_real - part_imag * hole_imag
    cell_imag = part_real * hole_imag + part_imag * hole_real
    mom_real, mom_imag = to_momenta(cell_real, cell_imag, cosine_table, sine_table)
    return jnp.stack([mom_real, mom_imag]).astype(jnp.bfloat16)


def product_of(left_side, right_side):
    return jnp.einsum("kij,kjl->kil", left_side, right_side, preferred_element_type=jnp.float32)


def complex_batched(left_real, left_imag, right_real, right_imag):
    real_out = product_of(left_real, right_real) - product_of(left_imag, right_imag)
    imag_out = product_of(left_real, right_imag) + product_of(left_imag, right_real)
    return (real_out, imag_out)


def body(green_particle, green_hole, coulomb):
    tile_rows = green_particle.shape[2]
    moved_part, moved_hole = (
        lax.all_to_all(green_particle, "kt", split_axis=3, concat_axis=1, tiled=True),
        lax.all_to_all(green_hole, "kt", split_axis=3, concat_axis=1, tiled=True),
    )
    points = moved_part.shape[1]
    narrow = moved_part.shape[3]
    polar_q = polarize(
        moved_part.reshape(2, points, tile_rows * narrow),
        moved_hole.reshape(2, points, tile_rows * narrow),
    )
    polar_q = polar_q.reshape(2, points, tile_rows, narrow)
    polar_rows = lax.all_to_all(polar_q, "kt", split_axis=1, concat_axis=3, tiled=True)
    mid_real, mid_imag = complex_batched(polar_rows[0], polar_rows[1], coulomb[0], coulomb[1])
    mid_stack = jnp.stack([mid_real.astype(jnp.bfloat16), mid_imag.astype(jnp.bfloat16)])
    row_start = lax.axis_index("tile") * tile_rows
    coulomb_rows = lax.dynamic_slice_in_dim(coulomb, row_start, tile_rows, 2)
    segment = lax.all_gather(mid_stack, "tile", axis=2, tiled=True)
    left_real = coulomb_rows[0]
    left_imag = coulomb_rows[1]
    more_real, more_imag = complex_batched(left_real, left_imag, segment[0], segment[1])
    summed = jnp.stack([more_real, more_imag])
    return coulomb_rows.astype(jnp.float32) + summed


def solution(mesh):
    return jax.shard_map(
        body,
        mesh=mesh,
        in_specs=(
            P(None, "kt", "tile", None),
            P(None, "kt", "tile", None),
            P(None, "kt", None, None),
        ),
        out_specs=P(None, "kt", "tile", None),
        check_vma=False,
    )
```

profile of v0, /device:TPU:0, one launch (start us, length us, event | category | flops | bytes accessed | tf_op | source)
XLA Modules:
  0.0 1116.9 jit_solution(6014429570869471573)
XLA Ops:
  6.5 12.6 %copy.8 = bf16[2,8,256,1024]{2,1,0,3:T(8,128)(2,1)} copy(bf16[2,8,256,1024]{3,2,1,0:T(8,128)(2,1)} %param.3) | data formatting | bytes 16777216 | tf_op args[0]
  19.1 7.3 all-to-all-start
  26.4 12.5 %copy.10 = bf16[2,8,256,1024]{2,1,0,3:T(8,128)(2,1)} copy(bf16[2,8,256,1024]{3,2,1,0:T(8,128)(2,1)} %param.4) | data formatting | bytes 16777216 | tf_op args[1]
  38.9 170.7 %all-to-all-done = bf16[2,8,256,1024]{2,1,0,3:T(8,128)(2,1)} async-done(((bf16[2,8,256,1024]{2,1,0,3:T(8,128)(2,1)}), bf16[2,8,256,1024]{2,1,0,3:T(8,128)(2,1)}, u32[]{:S(2)}, u32[]{:S(2)}) %all-to-all-start) | async-done | bytes 8388640 | tf_op jit(solution)/shard_map/all_to_all | solution.py:71
  209.6 5.0 all-to-all-start.1
  214.6 0.0 all-gather.2.cloned.1.call-start
  214.7 12.5 %copy.9 = bf16[2,8,256,8,128]{4,2,1,3,0:T(8,128)(2,1)} copy(bf16[2,8,256,8,128]{2,1,0,4,3:T(8,128)(2,1)} %bitcast.1) | data formatting | bytes 16777216 | tf_op jit(solution)/shard_map/all_to_all | solution.py:71
  227.2 5.3 slice_bitcast_fusion.8
  232.5 14.0 %fusion.28 = f32[64,32768]{1,0:T(8,128)} fusion(bf16[8,8,256,128]{3,2,1,0:T(8,128)(2,1)S(1)} %get-tuple-element.12, s32[64]{0:T(128)S(1)} %get-tuple-element.13, s32[64]{0:T(128)S(1)} %get-tuple-element.14, s32[64]{0:T(128)S(1)} %and_select_fusion.3), kind=kOutput, calls=%fused_computation.48 | convolution fusion | flops 1610690560 | bytes 12583680 | tf_op jit(solution)/shard_map/dot_general | solution.py:30
  246.5 14.5 %fusion.30 = f32[64,32768]{1,0:T(8,128)} fusion(bf16[8,8,256,128]{3,2,1,0:T(8,128)(2,1)S(1)} %get-tuple-element.12, s32[64]{0:T(128)S(1)} %get-tuple-element.13, s32[64]{0:T(128)S(1)} %get-tuple-element.14, s32[64]{0:T(128)S(1)} %and_select_fusion.3), kind=kOutput, calls=%fused_computation.50 | convolution fusion | flops 1610690560 | bytes 12583680 | tf_op jit(solution)/shard_map/dot_general | solution.py:28
  261.0 135.8 %all-to-all-done.1 = bf16[2,8,256,1024]{2,1,0,3:T(8,128)(2,1)} async-done(((bf16[2,8,256,1024]{2,1,0,3:T(8,128)(2,1)}), bf16[2,8,256,1024]{2,1,0,3:T(8,128)(2,1)}, u32[]{:S(2)}, u32[]{:S(2)}) %all-to-all-start.1) | async-done | bytes 8388640 | tf_op jit(solution)/shard_map/all_to_all | solution.py:72
  396.9 12.2 %copy.11 = bf16[2,8,256,8,128]{4,2,1,3,0:T(8,128)(2,1)} copy(bf16[2,8,256,8,128]{2,1,0,4,3:T(8,128)(2,1)} %bitcast.3) | data formatting | bytes 16777216 | tf_op jit(solution)/shard_map/all_to_all | solution.py:72
  409.1 4.0 slice_bitcast_fusion.6
  413.1 5.4 fusion.22
  418.4 5.4 fusion.24
  423.9 0.0 slice-start.2
  423.9 14.6 %convolution_add_fusion = f32[64,32768]{1,0:T(8,128)} fusion(f32[64,32768]{1,0:T(8,128)S(1)} %fusion.22, bf16[8,8,256,128]{3,2,1,0:T(8,128)(2,1)S(1)} %get-tuple-element.9, s32[64]{0:T(128)S(1)} %get-tuple-element.13, s32[64]{0:T(128)S(1)} %get-tuple-element.14, s32[64]{0:T(128)S(1)} %and_select_fusion.3), kind=kOutput, calls=%fused_computation | convolution fusion | flops 1612787712 | bytes 20972288 | tf_op jit(solution)/shard_map/dot_general | solution.py:31
  438.5 0.0 copy-start.1
  438.5 0.0 slice-start.3
  438.5 14.7 %convolution_subtract_fusion = f32[64,32768]{1,0:T(8,128)} fusion(f32[64,32768]{1,0:T(8,128)S(1)} %fusion.24, bf16[8,8,256,128]{3,2,1,0:T(8,128)(2,1)S(1)} %get-tuple-element.9, s32[64]{0:T(128)S(1)} %get-tuple-element.13, s32[64]{0:T(128)S(1)} %get-tuple-element.14, s32[64]{0:T(128)S(1)} %and_select_fusion.3), kind=kOutput, calls=%fused_computation.2 | convolution fusion | flops 1612787712 | bytes 20972288 | tf_op jit(solution)/shard_map/dot_general | solution.py:29
  453.2 0.0 slice-done.2
  453.2 0.0 copy-done.1
  453.3 0.0 slice-done.3
  453.3 14.4 %convolution_subtract_fusion.1 = f32[64,32768]{1,0:T(8,128)} fusion(f32[64,32768]{1,0:T(8,128)S(1)} %bitcast.119, bf16[8,8,256,128]{3,2,1,0:T(8,128)(2,1)S(1)} %copy-done.1, s32[64]{0:T(128)S(1)} %get-tuple-element.13, s32[64]{0:T(128)S(1)} %get-tuple-element.14, s32[64]{0:T(128)S(1)} %and_select_fusion.3), kind=kOutput, calls=%fused_computation.3 | convolution fusion | flops 1612787712 | bytes 20972288 | tf_op jit(solution)/shard_map/dot_general | solution.py:29
  467.7 22.5 %multiply_subtract_fusion = (f32[64,32768]{1,0:T(8,128)}, f32[64,32768]{1,0:T(8,128)}) fusion(f32[64,32768]{1,0:T(8,128)} %convolution_add_fusion, f32[64,32768]{1,0:T(8,128)} %convolution_subtract_fusion.1, f32[64,32768]{1,0:T(8,128)} %convolution_subtract_fusion, f32[64,32768]{1,0:T(8,128)} %fusion.28, bf16[8,8,256,128]{3,2,1,0:T(8,128)(2,1)} %get-tuple-element.11, ...), kind=kOutput, calls=%fused_computation.35 | convolution fusion | flops 1625370624 | bytes 54526720 | tf_op jit(solution)/shard_map/dot_general | solution.py:31
  490.2 0.0 copy-start
  490.2 12.3 %fusion.50 = f32[64,32768]{1,0:T(8,128)} fusion(f32[64,32768]{1,0:T(8,128)} %get-tuple-element.5, s32[64]{0:T(128)S(1)} %get-tuple-element.13, s32[64]{0:T(128)S(1)} %get-tuple-element.14, s32[64]{0:T(128)S(1)} %and_select_fusion.3), kind=kOutput, calls=%fused_computation.77 | convolution fusion | flops 1610690560 | bytes 16777984 | tf_op jit(solution)/shard_map/dot_general | solution.py:37
  502.5 0.0 copy-done
  502.5 0.0 slice-start
  502.6 7.8 fusion.49
  510.3 0.0 slice-start.1
  510.3 12.9 %fusion.45 = bf16[8,8,256,128]{3,1,2,0:T(8,128)(2,1)} fusion(f32[64,32768]{1,0:T(8,128)} %fusion.50, f32[64,32768]{1,0:T(8,128)S(1)} %copy-done, s32[64]{0:T(128)S(1)} %get-tuple-element.13, s32[64]{0:T(128)S(1)} %get-tuple-element.14, s32[64]{0:T(128)S(1)} %and_select_fusion.3), kind=kOutput, calls=%fused_computation.67 | convolution fusion | flops 1614884864 | bytes 20972288 | tf_op jit(solution)/shard_map/dot_general | solution.py:38
  523.3 0.0 slice-done
  523.3 0.0 slice-done.1
  523.3 8.9 fusion.44
  532.1 0.0 copy-start.2
  532.2 1.2 copy.20
  533.3 0.5 bitcast_bitcast_fusion
  533.8 0.5 copy-done.2
  534.3 1.2 copy.19
  535.5 2.2 bitcast_bitcast_fusion.1
  537.7 6.4 pad_maximum_fusion
  544.1 187.9 %all_to_all.45 = bf16[2,64,256,128]{3,2,0,1:T(8,128)(2,1)} all-to-all(bf16[2,64,256,128]{3,2,0,1:T(8,128)(2,1)} %pad_maximum_fusion), channel_id=1, replica_groups=mesh['kt'=8,'tile'=4] {'kt'}, dimensions={1} | all-to-all | bytes 16777216 | tf_op jit(solution)/shard_map/all_to_all | solution.py:81
  732.0 13.9 %copy.56 = bf16[2,8,8,256,128]{4,1,3,2,0:T(8,128)(2,1)} copy(bf16[2,8,8,256,128]{4,3,0,2,1:T(8,128)(2,1)} %bitcast.123) | data formatting | bytes 16777216 | tf_op jit(solution)/shard_map/all_to_all | solution.py:81
  745.9 5.8 fusion.116
  751.6 7.3 squeeze.43
  759.0 7.4 squeeze.41
  766.4 0.0 copy-start.3
  766.4 15.1 %fusion.2 = f32[8,256,1024]{2,1,0:T(8,128)} fusion(bf16[8,256,1024]{2,1,0:T(8,128)(2,1)} %squeeze.41, bf16[2,8,1024,1024]{3,2,1,0:T(8,128)(2,1)} %param.5), kind=kOutput, calls=%fused_computation.11 | convolution fusion | flops 4294967296 | bytes 29360128 | tf_op jit(solution)/shard_map/kij,kjl->kil/dot_general | solution.py:59
  781.5 0.0 copy-done.3
  781.5 13.6 %fusion.4 = f32[8,256,1024]{2,1,0:T(8,128)} fusion(bf16[8,256,1024]{2,1,0:T(8,128)(2,1)S(1)} %copy-done.3, bf16[2,8,1024,1024]{3,2,1,0:T(8,128)(2,1)} %param.5), kind=kOutput, calls=%fused_computation.13 | convolution fusion | flops 4294967296 | bytes 29360128 | tf_op jit(solution)/shard_map/kij,kjl->kil/dot_general | solution.py:59
  795.1 14.8 %fusion.19 = bf16[1,8,256,1024]{3,2,1,0:T(8,128)(2,1)} fusion(f32[8,256,1024]{2,1,0:T(8,128)} %fusion.2, bf16[8,256,1024]{2,1,0:T(8,128)(2,1)S(1)} %copy-done.3, bf16[2,8,1024,1024]{3,2,1,0:T(8,128)(2,1)} %param.5), kind=kOutput, calls=%fused_computation.37 | convolution fusion | flops 4299161600 | bytes 33554432 | tf_op jit(solution)/shard_map/kij,kjl->kil/dot_general | solution.py:59
  809.9 0.0 copy-start.4
  809.9 13.7 %fusion.18 = bf16[1,8,256,1024]{3,2,1,0:T(8,128)(2,1)} fusion(f32[8,256,1024]{2,1,0:T(8,128)} %fusion.4, bf16[8,256,1024]{2,1,0:T(8,128)(2,1)} %squeeze.41, bf16[2,8,1024,1024]{3,2,1,0:T(8,128)(2,1)} %param.5), kind=kOutput, calls=%fused_computation.36 | convolution fusion | flops 4299161600 | bytes 33554432 | tf_op jit(solution)/shard_map/kij,kjl->kil/dot_general | solution.py:59
  823.6 0.0 copy-done.4
  823.6 6.4 pad_maximum_fusion.1
  830.0 0.0 all-gather.2.cloned.1.call-update
  830.0 200.5 %all-gather.2.cloned.1.call-done = bf16[2,8,1024,1024]{3,2,1,0:T(8,128)(2,1)} async-done(((bf16[2,8,256,1024]{3,2,1,0:T(8,128)(2,1)}), bf16[2,8,1024,1024]{3,2,1,0:T(8,128)(2,1)}) %all-gather.2.cloned.1.call-update) | async-done | bytes 33554448 | tf_op jit(solution)/shard_map/all_gather | solution.py:86
  1030.5 14.8 %fusion.11 = f32[8,256,1024]{2,1,0:T(8,128)} fusion(bf16[2,8,1024,1024]{3,2,1,0:T(8,128)(2,1)} %all-gather.2.cloned.1.call-done, bf16[2,8,1024,1024]{3,2,1,0:T(8,128)(2,1)} %param.5, s32[]{:T(128)S(6)} %select_n.170), kind=kOutput, calls=%fused_computation.20 | convolution fusion | flops 4294967296 | bytes 29360132 | tf_op jit(solution)/shard_map/kij,kjl->kil/dot_general | solution.py:59
  1045.3 15.0 %fusion.10 = f32[8,256,1024]{2,1,0:T(8,128)} fusion(bf16[2,8,1024,1024]{3,2,1,0:T(8,128)(2,1)} %all-gather.2.cloned.1.call-done, bf16[2,8,1024,1024]{3,2,1,0:T(8,128)(2,1)} %param.5, s32[]{:T(128)S(6)} %add.203, s32[]{:T(128)S(6)} %select_n.170), kind=kOutput, calls=%fused_computation.19 | convolution fusion | flops 4294967296 | bytes 29360136 | tf_op jit(solution)/shard_map/kij,kjl->kil/dot_general | solution.py:59
  1060.3 17.2 %add_bitcast_fusion = f32[1,8,256,1024]{3,2,1,0:T(8,128)} fusion(f32[8,256,1024]{2,1,0:T(8,128)} %fusion.10, bf16[2,8,1024,1024]{3,2,1,0:T(8,128)(2,1)} %all-gather.2.cloned.1.call-done, bf16[2,8,1024,1024]{3,2,1,0:T(8,128)(2,1)} %param.5, s32[]{:T(128)S(6)} %select_n.170), kind=kOutput, calls=%fused_computation.30 | convolution fusion | flops 4297064448 | bytes 37748740 | tf_op jit(solution)/shard_map/kij,kjl->kil/dot_general | solution.py:59
  1077.5 17.5 %subtract_bitcast_fusion = f32[1,8,256,1024]{3,2,1,0:T(8,128)} fusion(f32[8,256,1024]{2,1,0:T(8,128)} %fusion.11, bf16[2,8,1024,1024]{3,2,1,0:T(8,128)(2,1)} %all-gather.2.cloned.1.call-done, bf16[2,8,1024,1024]{3,2,1,0:T(8,128)(2,1)} %param.5, s32[]{:T(128)S(6)} %add.203, s32[]{:T(128)S(6)} %select_n.170), kind=kOutput, calls=%fused_computation.31 | convolution fusion | flops 4297064448 | bytes 37748744 | tf_op jit(solution)/shard_map/kij,kjl->kil/dot_general | solution.py:59
  1095.0 14.7 %maximum_add_fusion = f32[2,8,256,1024]{3,2,1,0:T(8,128)} fusion(f32[1,8,256,1024]{3,2,1,0:T(8,128)} %add_bitcast_fusion, f32[1,8,256,1024]{3,2,1,0:T(8,128)} %subtract_bitcast_fusion, bf16[2,8,1024,1024]{3,2,1,0:T(8,128)(2,1)} %param.5, s32[]{:T(128)S(6)} %select_n.170), kind=kLoop, calls=%fused_computation.10 | loop fusion | flops 12582912 | bytes 41943044 | tf_op jit(solution)/shard_map/add | solution.py:91
  (4 shorter events, 0.0 us)
Async XLA Ops:
  19.1 190.5 %all-to-all-start = ((bf16[2,8,256,1024]{2,1,0,3:T(8,128)(2,1)}), bf16[2,8,256,1024]{2,1,0,3:T(8,128)(2,1)}, u32[]{:S(2)}, u32[]{:S(2)}) async-start(bf16[2,8,256,1024]{2,1,0,3:T(8,128)(2,1)} %copy.8), calls=%async_computation | async-start | bytes 16777216 | tf_op jit(solution)/shard_map/all_to_all | solution.py:71
  209.6 187.3 %all-to-all-start.1 = ((bf16[2,8,256,1024]{2,1,0,3:T(8,128)(2,1)}), bf16[2,8,256,1024]{2,1,0,3:T(8,128)(2,1)}, u32[]{:S(2)}, u32[]{:S(2)}) async-start(bf16[2,8,256,1024]{2,1,0,3:T(8,128)(2,1)} %copy.10), calls=%async_computation.1 | async-start | bytes 16777216 | tf_op jit(solution)/shard_map/all_to_all | solution.py:72
  214.6 815.9 %all-gather.2.cloned.1.call-start = ((), (), s32[]{:S(2)}) async-start(), calls=%async_computation.3 | async-start | bytes 41943040 | tf_op jit(solution)/shard_map/all_gather | solution.py:86
  423.9 29.4 %slice-start.2 = ((s8[8388608]{0:T(1024)(128)(4,1)}), s8[4194304]{0:T(1024)(128)(4,1)S(1)}, s32[]{:S(2)}) async-start(s8[8388608]{0:T(1024)(128)(4,1)} %bitcast.118), calls=%async_computation.6 | async-start | bytes 8388608
  438.5 14.8 %copy-start.1 = (bf16[8,8,256,128]{3,2,1,0:T(8,128)(2,1)S(1)}, bf16[8,8,256,128]{3,2,1,0:T(8,128)(2,1)}, u32[]{:S(2)}) copy-start(bf16[8,8,256,128]{3,2,1,0:T(8,128)(2,1)} %get-tuple-element.11) | copy-start | bytes 12582916
  438.5 14.8 %slice-start.3 = ((s8[8388608]{0:T(1024)(128)(4,1)}), s8[4194304]{0:T(1024)(128)(4,1)S(1)}, s32[]{:S(2)}) async-start(s8[8388608]{0:T(1024)(128)(4,1)} %bitcast.118), calls=%async_computation.7 | async-start | bytes 8388608
  490.2 12.3 %copy-start = (f32[64,32768]{1,0:T(8,128)S(1)}, f32[64,32768]{1,0:T(8,128)}, u32[]{:S(2)}) copy-start(f32[64,32768]{1,0:T(8,128)} %get-tuple-element.6) | copy-start | bytes 25165828
  502.5 20.7 %slice-start = ((s8[8388608]{0:T(1024)(128)(4,1)}), s8[4194304]{0:T(1024)(128)(4,1)S(1)}, s32[]{:S(2)}) async-start(s8[8388608]{0:T(1024)(128)(4,1)} %bitcast.116), calls=%async_computation.4 | async-start | bytes 8388608
  510.3 12.9 %slice-start.1 = ((s8[8388608]{0:T(1024)(128)(4,1)}), s8[4194304]{0:T(1024)(128)(4,1)S(1)}, s32[]{:S(2)}) async-start(s8[8388608]{0:T(1024)(128)(4,1)} %bitcast.116), calls=%async_computation.5 | async-start | bytes 8388608
  532.1 2.2 copy-start.2
  766.4 15.1 %copy-start.3 = (bf16[8,256,1024]{2,1,0:T(8,128)(2,1)S(1)}, bf16[8,256,1024]{2,1,0:T(8,128)(2,1)}, u32[]{:S(2)}) copy-start(bf16[8,256,1024]{2,1,0:T(8,128)(2,1)} %squeeze.43) | copy-start | bytes 12582916
  809.9 13.8 %copy-start.4 = (bf16[1,8,256,1024]{3,2,1,0:T(8,128)(2,1)S(1)}, bf16[1,8,256,1024]{3,2,1,0:T(8,128)(2,1)}, u32[]{:S(2)}) copy-start(bf16[1,8,256,1024]{3,2,1,0:T(8,128)(2,1)} %fusion.19) | copy-start | bytes 12582916
Sparse Core Ops, SparseCore 0:
  830.1 200.3 all-gather.1
where the time goes:
time: 1120 us
  waiting for transfers between devices  507 us (45%)
  matrix products  269 us (24%)
  blocking collectives  188 us (17%)
  local copies, waits for them, and re-layouts  99 us (9%)
  other arithmetic  27.4 us (2%)
  between operations  14 us (1%)
  starting transfers between devices  12.4 us (1%)
    all_gather x1, waiting for transfers between devices, body(): segment = lax.all_gather(mid_stack, 'tile', axis=2, tiled=True)  201 us
    all_to_all x1, blocking collectives, body(): lax.all_to_all(polar_q, 'kt', split_axis=1, concat_axis=3, tiled=True)  188 us
    all_to_all x1, waiting for transfers between devices, body(): lax.all_to_all(green_particle, 'kt', split_axis=3, concat_axis=1, tiled=T...  171 us
    all_to_all x1, waiting for transfers between devices, body(): lax.all_to_all(green_hole, 'kt', split_axis=3, concat_axis=1, tiled=True)  136 us
    dot_general x8, matrix products, product_of(): jnp.einsum('kij,kjl->kil', left_side, right_side, preferred_element_type=...  122 us
    unnamed x24, local copies, waits for them, and re-layouts  37.2 us
    dot_general x2, matrix products, to_cells(): jnp.dot(cosine_table, imag_part, precision=HIGHEST)  37.1 us
    dot_general x2, matrix products, to_cells(): jnp.dot(sine_table, imag_part, precision=HIGHEST)  29.1 us
  transfers between devices with their start and end apart: 3, of which 3 were waited for; matrix products, arithmetic and copies ran while one was open for 5% of the time, Pallas kernels for 0%

commit v1 on v0

--- a/solution.py
+++ b/solution.py
@@ -3,10 +3,17 @@
 import jax.numpy as jnp
 from jax import lax
 from jax.sharding import PartitionSpec as P
+from jax.lax import all_gather
 
 KSIDE = 4
 K = 64
 HIGHEST = lax.Precision.HIGHEST
+
+
+def report_threads(chunk):
+    t_next = all_gather(chunk, axis_name="tile")
+    row_out = jnp.concatenate(t_next, axis=2)
+    return row_out
 
 
 def phase_tables(points, side_count):
@@ -83,7 +90,7 @@
     mid_stack = jnp.stack([mid_real.astype(jnp.bfloat16), mid_imag.astype(jnp.bfloat16)])
     row_start = lax.axis_index("tile") * tile_rows
     coulomb_rows = lax.dynamic_slice_in_dim(coulomb, row_start, tile_rows, 2)
-    segment = lax.all_gather(mid_stack, "tile", axis=2, tiled=True)
+    segment = report_threads(mid_stack)
     left_real = coulomb_rows[0]
     left_imag = coulomb_rows[1]
     more_real, more_imag = complex_batched(left_real, left_imag, segment[0], segment[1])

time: 1120 us -> 1190 us (1.062)
  local copies, waits for them, and re-layouts: 99 us -> 151 us
  matrix products: 269 us -> 286 us
    all_to_all x1, waiting for transfers between devices: 136 us -> 171 us  [body(): lax.all_to_all(green_hole, 'kt', split_axis=3, concat_axis=1, tiled=True)]
    all_to_all x1, waiting for transfers between devices: 171 us -> 136 us  [body(): lax.all_to_all(green_particle, 'kt', split_axis=3, concat_axis=1, tiled=T...]
    slice x0 -> x1, local copies, waits for them, and re-layouts: none -> 23.3 us  [body(): segment[0]]
    all_gather x0 -> x1, local copies, waits for them, and re-layouts: none -> 23.2 us  [report_threads(): t_next = all_gather(chunk, axis_name='tile')]
    unnamed x24 -> x28, local copies, waits for them, and re-layouts: 37.2 us -> 42.9 us
where the time goes in v1:
time: 1190 us
  waiting for transfers between devices  507 us (43%)
  matrix products  286 us (24%)
  blocking collectives  188 us (16%)
  local copies, waits for them, and re-layouts  151 us (13%)
  other arithmetic  28.7 us (2%)
  between operations  14 us (1%)
  starting transfers between devices  12.3 us (1%)
    all_gather x1, waiting for transfers between devices, report_threads(): t_next = all_gather(chunk, axis_name='tile')  200 us
    all_to_all x1, blocking collectives, body(): lax.all_to_all(polar_q, 'kt', split_axis=1, concat_axis=3, tiled=True)  188 us
    all_to_all x1, waiting for transfers between devices, body(): lax.all_to_all(green_hole, 'kt', split_axis=3, concat_axis=1, tiled=True)  171 us
    all_to_all x1, waiting for transfers between devices, body(): lax.all_to_all(green_particle, 'kt', split_axis=3, concat_axis=1, tiled=T...  136 us
    dot_general x8, matrix products, product_of(): jnp.einsum('kij,kjl->kil', left_side, right_side, preferred_element_type=...  121 us
    unnamed x28, local copies, waits for them, and re-layouts  42.9 us
    dot_general x2, matrix products, to_cells(): jnp.dot(cosine_table, imag_part, precision=HIGHEST)  37 us
    dot_general x2, matrix products, to_cells(): jnp.dot(sine_table, imag_part, precision=HIGHEST)  31.4 us
  transfers between devices with their start and end apart: 3, of which 3 were waited for; matrix products, arithmetic and copies ran while one was open for 5% of the time, Pallas kernels for 0%

profile of v1, /device:TPU:0, one launch (start us, length us, event | category | flops | bytes accessed | tf_op | source)
XLA Modules:
  0.0 1187.0 jit_solution(14686254979678681340)
XLA Ops:
  6.5 12.5 %copy.14 = bf16[2,8,256,1024]{2,1,0,3:T(8,128)(2,1)} copy(bf16[2,8,256,1024]{3,2,1,0:T(8,128)(2,1)} %param.4) | data formatting | bytes 16777216 | tf_op args[1]
  19.0 7.3 all-to-all-start.1
  26.3 12.6 %copy.12 = bf16[2,8,256,1024]{2,1,0,3:T(8,128)(2,1)} copy(bf16[2,8,256,1024]{3,2,1,0:T(8,128)(2,1)} %param.3) | data formatting | bytes 16777216 | tf_op args[0]
  39.0 170.6 %all-to-all-done.1 = bf16[2,8,256,1024]{2,1,0,3:T(8,128)(2,1)} async-done(((bf16[2,8,256,1024]{2,1,0,3:T(8,128)(2,1)}), bf16[2,8,256,1024]{2,1,0,3:T(8,128)(2,1)}, u32[]{:S(2)}, u32[]{:S(2)}) %all-to-all-start.1) | async-done | bytes 8388640 | tf_op jit(solution)/shard_map/all_to_all | solution.py:79
  209.5 5.0 all-to-all-start
  214.5 0.0 all-gather.3.cloned.1.call-start
  214.5 12.3 %copy.15 = bf16[2,8,256,8,128]{4,2,1,3,0:T(8,128)(2,1)} copy(bf16[2,8,256,8,128]{2,1,0,4,3:T(8,128)(2,1)} %bitcast.3) | data formatting | bytes 16777216 | tf_op jit(solution)/shard_map/all_to_all | solution.py:79
  226.8 5.3 slice_bitcast_fusion
  232.1 14.0 %fusion.20 = f32[64,32768]{1,0:T(8,128)} fusion(bf16[8,8,256,128]{3,2,1,0:T(8,128)(2,1)S(1)} %get-tuple-element.12, s32[64]{0:T(128)S(1)} %get-tuple-element.15, s32[64]{0:T(128)S(1)} %get-tuple-element.16, s32[64]{0:T(128)S(1)} %and_select_fusion.3), kind=kOutput, calls=%fused_computation.39 | convolution fusion | flops 1610690560 | bytes 12583680 | tf_op jit(solution)/shard_map/dot_general | solution.py:35
  246.1 14.6 %fusion.18 = f32[64,32768]{1,0:T(8,128)} fusion(bf16[8,8,256,128]{3,2,1,0:T(8,128)(2,1)S(1)} %get-tuple-element.12, s32[64]{0:T(128)S(1)} %get-tuple-element.15, s32[64]{0:T(128)S(1)} %get-tuple-element.16, s32[64]{0:T(128)S(1)} %and_select_fusion.3), kind=kOutput, calls=%fused_computation.37 | convolution fusion | flops 1610690560 | bytes 12583680 | tf_op jit(solution)/shard_map/dot_general | solution.py:37
  260.7 136.0 %all-to-all-done = bf16[2,8,256,1024]{2,1,0,3:T(8,128)(2,1)} async-done(((bf16[2,8,256,1024]{2,1,0,3:T(8,128)(2,1)}), bf16[2,8,256,1024]{2,1,0,3:T(8,128)(2,1)}, u32[]{:S(2)}, u32[]{:S(2)}) %all-to-all-start) | async-done | bytes 8388640 | tf_op jit(solution)/shard_map/all_to_all | solution.py:78
  396.7 12.3 %copy.13 = bf16[2,8,256,8,128]{4,2,1,3,0:T(8,128)(2,1)} copy(bf16[2,8,256,8,128]{2,1,0,4,3:T(8,128)(2,1)} %bitcast.1) | data formatting | bytes 16777216 | tf_op jit(solution)/shard_map/all_to_all | solution.py:78
  409.0 0.0 slice-start.4
  409.1 3.9 slice_bitcast_fusion.2
  413.0 0.0 copy-start.1
  413.0 0.0 slice-start.5
  413.0 14.3 %fusion.26 = f32[64,32768]{1,0:T(8,128)} fusion(bf16[8,8,256,128]{3,2,1,0:T(8,128)(2,1)S(1)} %get-tuple-element.14, s32[64]{0:T(128)S(1)} %get-tuple-element.15, s32[64]{0:T(128)S(1)} %get-tuple-element.16, s32[64]{0:T(128)S(1)} %and_select_fusion.3), kind=kOutput, calls=%fused_computation.45 | convolution fusion | flops 1610690560 | bytes 12583680 | tf_op jit(solution)/shard_map/dot_general | solution.py:35
  427.3 14.1 %fusion.24 = f32[64,32768]{1,0:T(8,128)} fusion(bf16[8,8,256,128]{3,2,1,0:T(8,128)(2,1)S(1)} %get-tuple-element.14, s32[64]{0:T(128)S(1)} %get-tuple-element.15, s32[64]{0:T(128)S(1)} %get-tuple-element.16, s32[64]{0:T(128)S(1)} %and_select_fusion.3), kind=kOutput, calls=%fused_computation.43 | convolution fusion | flops 1610690560 | bytes 12583680 | tf_op jit(solution)/shard_map/dot_general | solution.py:37
  441.4 0.0 slice-done.4
  441.4 0.0 slice-done.5
  441.4 0.0 copy-done.2
  441.4 0.0 slice-start.3
  441.4 14.7 %convolution_subtract_fusion = f32[64,32768]{1,0:T(8,128)} fusion(f32[64,32768]{1,0:T(8,128)S(1)} %bitcast.125, bf16[8,8,256,128]{3,2,1,0:T(8,128)(2,1)S(1)} %copy-done.2, s32[64]{0:T(128)S(1)} %get-tuple-element.15, s32[64]{0:T(128)S(1)} %get-tuple-element.16, s32[64]{0:T(128)S(1)} %and_select_fusion.3), kind=kOutput, calls=%fused_computation.2 | convolution fusion | flops 1612787712 | bytes 20972288 | tf_op jit(solution)/shard_map/dot_general | solution.py:36
  456.1 0.0 slice-done.2
  456.1 0.0 slice-done.3
  456.1 14.4 %convolution_add_fusion = f32[64,32768]{1,0:T(8,128)} fusion(f32[64,32768]{1,0:T(8,128)S(1)} %bitcast.123, bf16[8,8,256,128]{3,2,1,0:T(8,128)(2,1)S(1)} %copy-done.2, s32[64]{0:T(128)S(1)} %get-tuple-element.15, s32[64]{0:T(128)S(1)} %get-tuple-element.16, s32[64]{0:T(128)S(1)} %and_select_fusion.3), kind=kOutput, calls=%fused_computation | convolution fusion | flops 1612787712 | bytes 20972288 | tf_op jit(solution)/shard_map/dot_general | solution.py:38
  470.5 0.0 copy-done.1
  470.5 16.7 %convolution_subtract_fusion.1 = f32[64,32768]{1,0:T(8,128)} fusion(f32[64,32768]{1,0:T(8,128)} %fusion.26, bf16[8,8,256,128]{3,2,1,0:T(8,128)(2,1)S(1)} %get-tuple-element.13, s32[64]{0:T(128)S(1)} %get-tuple-element.15, s32[64]{0:T(128)S(1)} %get-tuple-element.16, s32[64]{0:T(128)S(1)} %and_select_fusion.3), kind=kOutput, calls=%fused_computation.3 | convolution fusion | flops 1612787712 | bytes 20972288 | tf_op jit(solution)/shard_map/dot_general | solution.py:36
  487.3 22.6 %multiply_subtract_fusion = (f32[64,32768]{1,0:T(8,128)}, f32[64,32768]{1,0:T(8,128)}) fusion(f32[64,32768]{1,0:T(8,128)} %convolution_add_fusion, f32[64,32768]{1,0:T(8,128)} %convolution_subtract_fusion.1, f32[64,32768]{1,0:T(8,128)} %convolution_subtract_fusion, f32[64,32768]{1,0:T(8,128)} %fusion.24, bf16[8,8,256,128]{3,2,1,0:T(8,128)(2,1)} %copy-done.1, ...), kind=kOutput, calls=%fused_computation.30 | convolution fusion | flops 1625370624 | bytes 54526720 | tf_op jit(solution)/shard_map/dot_general | solution.py:38
  509.8 10.4 fusion.50
  520.2 0.0 copy-done
  520.2 7.8 fusion.49
  528.0 10.6 fusion.45
  538.6 3.5 copy.24
  542.1 0.0 slice-start.1
  542.1 0.5 bitcast_bitcast_fusion.1
  542.6 0.0 slice-done
  542.6 1.7 slice-done.1
  544.3 10.4 fusion.44
  554.7 3.3 copy.25
  558.0 2.2 bitcast_bitcast_fusion
  560.3 6.4 pad_maximum_fusion
  566.7 187.9 %all_to_all.45 = bf16[2,64,256,128]{3,2,0,1:T(8,128)(2,1)} all-to-all(bf16[2,64,256,128]{3,2,0,1:T(8,128)(2,1)} %pad_maximum_fusion), channel_id=1, replica_groups=mesh['kt'=8,'tile'=4] {'kt'}, dimensions={1} | all-to-all | bytes 16777216 | tf_op jit(solution)/shard_map/all_to_all | solution.py:88
  754.6 13.9 %copy.63 = bf16[2,8,8,256,128]{4,1,3,2,0:T(8,128)(2,1)} copy(bf16[2,8,8,256,128]{4,3,0,2,1:T(8,128)(2,1)} %bitcast.129) | data formatting | bytes 16777216 | tf_op jit(solution)/shard_map/all_to_all | solution.py:88
  768.5 5.9 fusion.117
  774.3 7.3 squeeze.43
  781.6 7.4 squeeze.41
  789.1 0.0 copy-start.4
  789.1 15.0 %fusion.4 = f32[8,256,1024]{2,1,0:T(8,128)} fusion(bf16[8,256,1024]{2,1,0:T(8,128)(2,1)} %squeeze.43, bf16[2,8,1024,1024]{3,2,1,0:T(8,128)(2,1)} %param.5), kind=kOutput, calls=%fused_computation.12 | convolution fusion | flops 4294967296 | bytes 29360128 | tf_op jit(solution)/shard_map/kij,kjl->kil/dot_general | solution.py:66
  804.1 0.0 copy-done.4
  804.1 13.7 %fusion.2 = f32[8,256,1024]{2,1,0:T(8,128)} fusion(bf16[8,256,1024]{2,1,0:T(8,128)(2,1)S(1)} %copy-done.4, bf16[2,8,1024,1024]{3,2,1,0:T(8,128)(2,1)} %param.5), kind=kOutput, calls=%fused_computation.10 | convolution fusion | flops 4294967296 | bytes 29360128 | tf_op jit(solution)/shard_map/kij,kjl->kil/dot_general | solution.py:66
  817.8 13.4 %fusion.14 = bf16[1,8,256,1024]{3,2,1,0:T(8,128)(2,1)} fusion(f32[8,256,1024]{2,1,0:T(8,128)} %fusion.4, bf16[8,256,1024]{2,1,0:T(8,128)(2,1)} %squeeze.41, bf16[2,8,1024,1024]{3,2,1,0:T(8,128)(2,1)} %param.5), kind=kOutput, calls=%fused_computation.31 | convolution fusion | flops 4299161600 | bytes 33554432 | tf_op jit(solution)/shard_map/kij,kjl->kil/dot_general | solution.py:66
  831.2 0.0 copy-done.3
  831.2 14.8 %fusion.15 = bf16[1,8,256,1024]{3,2,1,0:T(8,128)(2,1)} fusion(f32[8,256,1024]{2,1,0:T(8,128)} %fusion.2, bf16[8,256,1024]{2,1,0:T(8,128)(2,1)S(1)} %copy-done.3, bf16[2,8,1024,1024]{3,2,1,0:T(8,128)(2,1)} %param.5), kind=kOutput, calls=%fused_computation.32 | convolution fusion | flops 4299161600 | bytes 33554432 | tf_op jit(solution)/shard_map/kij,kjl->kil/dot_general | solution.py:66
  845.9 7.6 pad_maximum_fusion.1
  853.6 0.0 all-gather.3.cloned.1.call-update
  853.6 200.4 %all-gather.3.cloned.1.call-done = bf16[8,8,256,1024]{3,2,1,0:T(8,128)(2,1)} async-done(((bf16[2,8,256,1024]{3,2,1,0:T(8,128)(2,1)}), bf16[8,8,256,1024]{3,2,1,0:T(8,128)(2,1)}) %all-gather.3.cloned.1.call-update) | async-done | bytes 33554448 | tf_op jit(solution)/shard_map/all_gather | solution.py:14
  1054.0 23.2 %copy.62 = bf16[4,2,8,256,1024]{4,3,0,2,1:T(8,128)(2,1)} copy(bf16[4,2,8,256,1024]{4,3,2,1,0:T(8,128)(2,1)} %bitcast.121) | data formatting | bytes 67108864 | tf_op jit(solution)/shard_map/all_gather | solution.py:14
  1077.3 23.3 %fusion.116 = (bf16[1,8,4,256,1024]{4,3,2,1,0:T(8,128)(2,1)}, bf16[1,8,4,256,1024]{4,3,2,1,0:T(8,128)(2,1)}) fusion(bf16[2,8,4,256,1024]{4,3,2,1,0:T(8,128)(2,1)} %bitcast.118), kind=kLoop, calls=%fused_computation.153 | loop fusion | bytes 67108864 | tf_op jit(solution)/shard_map/slice | solution.py:96
  1100.6 14.8 %fusion.37 = f32[8,256,1024]{2,1,0:T(8,128)} fusion(bf16[8,1024,1024]{2,1,0:T(8,128)(2,1)} %bitcast.114, bf16[2,8,1024,1024]{3,2,1,0:T(8,128)(2,1)} %param.5, s32[]{:T(128)S(6)} %select_n.170), kind=kOutput, calls=%fused_computation.62 | convolution fusion | flops 4294967296 | bytes 29360132 | tf_op jit(solution)/shard_map/kij,kjl->kil/dot_general | solution.py:66
  1115.4 14.8 %fusion.36 = f32[8,256,1024]{2,1,0:T(8,128)} fusion(bf16[8,1024,1024]{2,1,0:T(8,128)(2,1)} %bitcast.116, bf16[2,8,1024,1024]{3,2,1,0:T(8,128)(2,1)} %param.5, s32[]{:T(128)S(6)} %select_n.170), kind=kOutput, calls=%fused_computation.61 | convolution fusion | flops 4294967296 | bytes 29360132 | tf_op jit(solution)/shard_map/kij,kjl->kil/dot_general | solution.py:66
  1130.3 17.2 %subtract_bitcast_fusion = f32[1,8,256,1024]{3,2,1,0:T(8,128)} fusion(f32[8,256,1024]{2,1,0:T(8,128)} %fusion.37, bf16[8,1024,1024]{2,1,0:T(8,128)(2,1)} %bitcast.117, bf16[2,8,1024,1024]{3,2,1,0:T(8,128)(2,1)} %param.5, s32[]{:T(128)S(6)} %add.203, s32[]{:T(128)S(6)} %select_n.170), kind=kOutput, calls=%fused_computation.26 | convolution fusion | flops 4297064448 | bytes 37748744 | tf_op jit(solution)/shard_map/kij,kjl->kil/dot_general | solution.py:66
  1147.5 17.6 %add_bitcast_fusion = f32[1,8,256,1024]{3,2,1,0:T(8,128)} fusion(f32[8,256,1024]{2,1,0:T(8,128)} %fusion.36, bf16[8,1024,1024]{2,1,0:T(8,128)(2,1)} %bitcast.115, bf16[2,8,1024,1024]{3,2,1,0:T(8,128)(2,1)} %param.5, s32[]{:T(128)S(6)} %add.203, s32[]{:T(128)S(6)} %select_n.170), kind=kOutput, calls=%fused_computation.25 | convolution fusion | flops 4297064448 | bytes 37748744 | tf_op jit(solution)/shard_map/kij,kjl->kil/dot_general | solution.py:66
  1165.0 14.7 %maximum_add_fusion = f32[2,8,256,1024]{3,2,1,0:T(8,128)} fusion(f32[1,8,256,1024]{3,2,1,0:T(8,128)} %add_bitcast_fusion, f32[1,8,256,1024]{3,2,1,0:T(8,128)} %subtract_bitcast_fusion, bf16[2,8,1024,1024]{3,2,1,0:T(8,128)(2,1)} %param.5, s32[]{:T(128)S(6)} %select_n.170), kind=kLoop, calls=%fused_computation.9 | loop fusion | flops 12582912 | bytes 41943044 | tf_op jit(solution)/shard_map/add | solution.py:98
  (10 shorter events, 0.0 us)
Async XLA Ops:
  19.0 190.5 %all-to-all-start.1 = ((bf16[2,8,256,1024]{2,1,0,3:T(8,128)(2,1)}), bf16[2,8,256,1024]{2,1,0,3:T(8,128)(2,1)}, u32[]{:S(2)}, u32[]{:S(2)}) async-start(bf16[2,8,256,1024]{2,1,0,3:T(8,128)(2,1)} %copy.14), calls=%async_computation.1 | async-start | bytes 16777216 | tf_op jit(solution)/shard_map/all_to_all | solution.py:79
  209.5 187.2 %all-to-all-start = ((bf16[2,8,256,1024]{2,1,0,3:T(8,128)(2,1)}), bf16[2,8,256,1024]{2,1,0,3:T(8,128)(2,1)}, u32[]{:S(2)}, u32[]{:S(2)}) async-start(bf16[2,8,256,1024]{2,1,0,3:T(8,128)(2,1)} %copy.12), calls=%async_computation | async-start | bytes 16777216 | tf_op jit(solution)/shard_map/all_to_all | solution.py:78
  214.5 839.6 %all-gather.3.cloned.1.call-start = ((), (), s32[]{:S(2)}) async-start(), calls=%async_computation.3 | async-start | bytes 41943040 | tf_op jit(solution)/shard_map/all_gather | solution.py:14
  409.0 32.4 %slice-start.4 = ((s8[8388608]{0:T(1024)(128)(4,1)}), s8[4194304]{0:T(1024)(128)(4,1)S(1)}, s32[]{:S(2)}) async-start(s8[8388608]{0:T(1024)(128)(4,1)} %bitcast.124), calls=%async_computation.8 | async-start | bytes 8388608
  413.0 57.5 %copy-start.1 = (bf16[8,8,256,128]{3,2,1,0:T(8,128)(2,1)}, bf16[8,8,256,128]{3,2,1,0:T(8,128)(2,1)S(1)}, u32[]{:S(2)}) copy-start(bf16[8,8,256,128]{3,2,1,0:T(8,128)(2,1)S(1)} %get-tuple-element.13) | copy-start | bytes 12582916
  413.0 28.4 %slice-start.5 = ((s8[8388608]{0:T(1024)(128)(4,1)}), s8[4194304]{0:T(1024)(128)(4,1)S(1)}, s32[]{:S(2)}) async-start(s8[8388608]{0:T(1024)(128)(4,1)} %bitcast.124), calls=%async_computation.9 | async-start | bytes 8388608
  427.3 14.1 %copy-start.2 = (bf16[8,8,256,128]{3,2,1,0:T(8,128)(2,1)S(1)}, bf16[8,8,256,128]{3,2,1,0:T(8,128)(2,1)}, u32[]{:S(2)}) copy-start(bf16[8,8,256,128]{3,2,1,0:T(8,128)(2,1)} %get-tuple-element.11) | copy-start | bytes 12582916
  427.3 28.8 %slice-start.2 = ((s8[8388608]{0:T(1024)(128)(4,1)}), s8[4194304]{0:T(1024)(128)(4,1)S(1)}, s32[]{:S(2)}) async-start(s8[8388608]{0:T(1024)(128)(4,1)} %bitcast.122), calls=%async_computation.6 | async-start | bytes 8388608
  441.4 14.7 %slice-start.3 = ((s8[8388608]{0:T(1024)(128)(4,1)}), s8[4194304]{0:T(1024)(128)(4,1)S(1)}, s32[]{:S(2)}) async-start(s8[8388608]{0:T(1024)(128)(4,1)} %bitcast.122), calls=%async_computation.7 | async-start | bytes 8388608
  509.8 10.4 copy-start
  538.6 4.0 slice-start
  542.1 2.2 slice-start.1
  789.1 15.0 %copy-start.4 = (bf16[8,256,1024]{2,1,0:T(8,128)(2,1)S(1)}, bf16[8,256,1024]{2,1,0:T(8,128)(2,1)}, u32[]{:S(2)}) copy-start(bf16[8,256,1024]{2,1,0:T(8,128)(2,1)} %squeeze.41) | copy-start | bytes 12582916
  817.8 13.4 %copy-start.3 = (bf16[8,256,1024]{2,1,0:T(8,128)(2,1)S(1)}, bf16[8,256,1024]{2,1,0:T(8,128)(2,1)}, u32[]{:S(2)}) copy-start(bf16[8,256,1024]{2,1,0:T(8,128)(2,1)} %squeeze.43) | copy-start | bytes 12582916
Sparse Core Ops, SparseCore 0:
  853.7 200.2 all-gather.2
